TPU v7x, 32 devices: a whole 2x2x4 slice. The times are simulated.
32 devices in a mesh: row: 8 (over y, x, core), col: 4 (over z).
Axes of the slice: x: 2, y: 2, z: 4, core: 2. Of those that a mesh axis runs over, the one named last changes fastest.
Arguments:
- query_proj: bfloat16 [192, 192, 128], P('row', 'col'), may hold values from -8 to 8
- key_proj: bfloat16 [192, 192, 128], P('row', 'col'), may hold values from -8 to 8
- value_proj: bfloat16 [192, 192, 128], P('row', 'col'), may hold values from -6 to 6
- pair_bias: bfloat16 [4, 192, 192], P(None, 'col', 'row'), may hold values from -9 to 9
- pair_mask: int32 [192, 192], P('row', 'col'), may hold values 0 or 1
- grad_out: bfloat16 [192, 192, 128], P('row', 'col'), may hold values from -18 to 18
Outputs:
- grad_query: bfloat16 [192, 192, 128], P('row', 'col')
- grad_key: bfloat16 [192, 192, 128], P('row', 'col')
- grad_value: bfloat16 [192, 192, 128], P('row', 'col')
- grad_bias: float32 [4, 192, 192], P(None, 'col', 'row')
All inputs are finite; a program needn't handle non-finite values. No bound on the sum of `pair_mask` on one device may be relied on, other than what follows from the above.
Results may differ from a plain program's by a relative error of at most 0.0096.
Values may be sent and summed in bfloat16 or wider, within the bound.
A program may use at most 128 MiB of HBM per device.

v0:
```python
import math
import jax
import jax.numpy as jnp
from jax import lax
from jax.sharding import PartitionSpec as P

HEADS = 4
HEAD_DIM = 32


def block_grads(queries, keys_all, values_all, grads, mask_all, bias_full):
    block_rows, query_count, channel_count = queries.shape
    key_count = keys_all.shape[1]
    scale = 1.0 / math.sqrt(HEAD_DIM)
    query_heads = queries.reshape(block_rows, query_count, HEADS, HEAD_DIM)
    key_heads = keys_all.reshape(block_rows, key_count, HEADS, HEAD_DIM)
    value_heads = values_all.reshape(block_rows, key_count, HEADS, HEAD_DIM)
    grad_heads = grads.reshape(block_rows, query_count, HEADS, HEAD_DIM)
    masked = 1000000000.0 * (mask_all.astype(jnp.float32) - 1.0)
    scores = (
        jnp.einsum("bjhd,bkhd->bhjk", query_heads, key_heads, preferred_element_type=jnp.float32)
        * scale
    )
    scores = scores + bias_full.astype(jnp.float32)[None] + masked[:, None, None, :]
    top_score = jnp.max(scores, axis=-1, keepdims=True)
    weights = jnp.exp(scores - top_score)
    attn_probs = weights / jnp.sum(weights, axis=-1, keepdims=True)
    attn_low = attn_probs.astype(jnp.bfloat16)
    attended = jnp.einsum(
        "bhjk,bkhd->bjhd", attn_low, value_heads, preferred_element_type=jnp.float32
    )
    row_delta = jnp.sum(grad_heads.astype(jnp.float32) * attended, axis=-1)
    grad_probs = jnp.einsum(
        "bjhd,bkhd->bhjk", grad_heads, value_heads, preferred_element_type=jnp.float32
    )
    grad_scores = attn_probs * (grad_probs - jnp.transpose(row_delta, (0, 2, 1))[..., None])
    scores_low = grad_scores.astype(jnp.bfloat16)
    grad_queries = (
        jnp.einsum("bhjk,bkhd->bjhd", scores_low, key_heads, preferred_element_type=jnp.float32)
        * scale
    )
    grad_keys = (
        jnp.einsum("bhjk,bjhd->bkhd", scores_low, query_heads, preferred_element_type=jnp.float32)
        * scale
    )
    grad_values = jnp.einsum(
        "bhjk,bjhd->bkhd", attn_low, grad_heads, preferred_element_type=jnp.float32
    )
    bias_grad = jnp.sum(grad_scores, axis=0)
    return (
        grad_queries.reshape(block_rows, query_count, channel_count),
        grad_keys.reshape(block_rows, key_count, channel_count),
        grad_values.reshape(block_rows, key_count, channel_count),
        bias_grad,
    )


def all_blocks(queries, keys_all, values_all, grads, mask_all, bias_full):
    row_count, query_count, channel_count = queries.shape
    key_count = keys_all.shape[1]
    block_rows = 1
    while (
        block_rows * 2 <= row_count
        and row_count % (block_rows * 2) == 0
        and (block_rows * query_count < 512)
    ):
        block_rows = block_rows * 2
    steps_count = row_count // block_rows

    def split_rows(array):
        return array.reshape((steps_count, block_rows) + array.shape[1:])

    def one_block(bias_sum, pieces):
        grad_queries, grad_keys, grad_values, bias_grad = block_grads(
            pieces[0], pieces[1], pieces[2], pieces[3], pieces[4], bias_full
        )
        return (bias_sum + bias_grad, (grad_queries, grad_keys, grad_values))

    start_sum = jnp.zeros((HEADS, query_count, key_count), jnp.float32)
    bias_sum, stacked = lax.scan(
        one_block,
        start_sum,
        (
            split_rows(queries),
            split_rows(keys_all),
            split_rows(values_all),
            split_rows(grads),
            split_rows(mask_all),
        ),
    )
    return (
        stacked[0].reshape(row_count, query_count, channel_count),
        stacked[1].reshape(row_count, key_count, channel_count),
        stacked[2].reshape(row_count, key_count, channel_count),
        bias_sum,
    )


def local(query_proj, key_proj, value_proj, pair_bias, pair_mask, grad_out):
    bias_rows = lax.all_gather(pair_bias, "row", axis=2, tiled=True)
    mask_low = pair_mask.astype(jnp.bfloat16)
    local_tiles = (
        lax.all_to_all(query_proj, "col", split_axis=0, concat_axis=1, tiled=True),
        lax.all_to_all(key_proj, "col", split_axis=0, concat_axis=1, tiled=True),
        lax.all_to_all(value_proj, "col", split_axis=0, concat_axis=1, tiled=True),
        lax.all_to_all(grad_out, "col", split_axis=0, concat_axis=1, tiled=True),
        lax.all_to_all(mask_low, "col", split_axis=0, concat_axis=1, tiled=True),
    )
    bias_full = lax.all_gather(bias_rows, "col", axis=1, tiled=True)
    grad_queries, grad_keys, grad_values, bias_whole = all_blocks(
        local_tiles[0], local_tiles[1], local_tiles[2], local_tiles[3], local_tiles[4], bias_full
    )
    grad_query, grad_key, grad_value = (
        lax.all_to_all(
            grad_queries.astype(jnp.bfloat16), "col", split_axis=1, concat_axis=0, tiled=True
        ),
        lax.all_to_all(
            grad_keys.astype(jnp.bfloat16), "col", split_axis=1, concat_axis=0, tiled=True
        ),
        lax.all_to_all(
            grad_values.astype(jnp.bfloat16), "col", split_axis=1, concat_axis=0, tiled=True
        ),
    )
    bias_part = lax.psum_scatter(bias_whole, "col", scatter_dimension=1, tiled=True)
    grad_bias = lax.psum_scatter(bias_part, "row", scatter_dimension=2, tiled=True)
    return (grad_query, grad_key, grad_value, grad_bias)


def solution(mesh):
    placed = (
        P("row", "col", None),
        P("row", "col", None),
        P("row", "col", None),
        P(None, "col", "row"),
        P("row", "col"),
        P("row", "col", None),
    )
    return jax.shard_map(
        local,
        mesh=mesh,
        in_specs=placed,
        out_specs=(
            P("row", "col", None),
            P("row", "col", None),
            P("row", "col", None),
            P(None, "col", "row"),
        ),
        check_vma=False,
    )
```

profile of v0, /device:TPU:0, one launch (start us, length us, event | category | flops | bytes accessed | tf_op | source)
XLA Modules:
  0.0 196.8 jit_solution(4565069296105848895)
XLA Ops:
  8.0 11.7 %all_to_all.130 = bf16[4,2,144]{2,1,0:T(2,128)(2,1)S(1)} all-to-all(bf16[4,2,144]{2,1,0:T(2,128)(2,1)S(1)} %reshape.104), channel_id=1, replica_groups=mesh['row'=8,'col'=4] {'col'}, dimensions={0} | all-to-all | bytes 4608 | tf_op jit(solution)/shard_map/all_to_all | solution.py:107
  19.7 11.8 %all_to_all.131 = bf16[24,48,128]{2,1,0:T(8,128)(2,1)S(1)} all-to-all(bf16[24,48,128]{2,1,0:T(8,128)(2,1)} %param.8), channel_id=1, replica_groups=mesh['row'=8,'col'=4] {'col'}, dimensions={0} | all-to-all | bytes 589824 | tf_op jit(solution)/shard_map/all_to_all | solution.py:103
  31.6 11.7 %all_to_all.132 = bf16[24,48,128]{2,1,0:T(8,128)(2,1)S(1)} all-to-all(bf16[24,48,128]{2,1,0:T(8,128)(2,1)} %param.9), channel_id=1, replica_groups=mesh['row'=8,'col'=4] {'col'}, dimensions={0} | all-to-all | bytes 589824 | tf_op jit(solution)/shard_map/all_to_all | solution.py:104
  43.3 11.6 %all_to_all.133 = bf16[24,48,128]{2,1,0:T(8,128)(2,1)S(1)} all-to-all(bf16[24,48,128]{2,1,0:T(8,128)(2,1)} %param.10), channel_id=1, replica_groups=mesh['row'=8,'col'=4] {'col'}, dimensions={0} | all-to-all | bytes 589824 | tf_op jit(solution)/shard_map/all_to_all | solution.py:105
  54.9 3.5 %all-to-all-start.3 = ((bf16[24,48,128]{2,1,0:T(8,128)(2,1)}), bf16[24,48,128]{2,1,0:T(8,128)(2,1)S(1)}, u32[]{:S(2)}, u32[]{:S(2)}) async-start(bf16[24,48,128]{2,1,0:T(8,128)(2,1)} %param.13), calls=%async_computation.3 | async-start | bytes 589824 | tf_op jit(solution)/shard_map/all_to_all | solution.py:106
  58.5 9.3 %all_gather.6 = bf16[4,48,192]{1,0,2:T(4,128)(2,1)S(1)} all-gather(bf16[4,48,24]{1,0,2:T(4,128)(2,1)S(1)} %copy.115), channel_id=1, replica_groups=mesh['row'=8,'col'=4] {'row'}, dimensions={2}, use_global_device_ids=true | all-gather | bytes 82944 | tf_op jit(solution)/shard_map/all_gather | solution.py:100
  67.9 15.1 %all_gather.7 = bf16[4,192,192]{2,0,1:T(4,128)(2,1)S(1)} all-gather(bf16[4,48,192]{2,0,1:T(4,128)(2,1)S(1)} %copy.116), channel_id=1, replica_groups=mesh['row'=8,'col'=4] {'col'}, dimensions={1}, use_global_device_ids=true | all-gather | bytes 368640 | tf_op jit(solution)/shard_map/all_gather | solution.py:109
  84.4 23.5 %while.19 = (s32[]{:T(128)}, f32[4,192,192]{1,2,0:T(8,128)S(1)}, bf16[3,2,192,128]{3,2,1,0:T(8,128)(2,1)}, bf16[3,2,192,128]{3,2,1,0:T(8,128)(2,1)}, bf16[3,2,19...) while((s32[]{:T(128)}, f32[4,192,192]{1,2,0:T(8,128)S(1)}, ...), condition=%wide.region_5.6_spmd.clone, body=%wide.region_0.5_spmd.clone.sunk | while | flops 117423936 | bytes 24709288 | solution.py:80
  84.5 0.9 copy.164
  85.7 0.9 constant_dynamic-slice_fusion.10
  86.8 0.8 fusion.54
  92.3 0.9 copy.164
  93.5 0.9 constant_dynamic-slice_fusion.10
  94.7 0.8 fusion.54
  100.2 0.9 copy.164
  101.4 0.9 constant_dynamic-slice_fusion.10
  102.5 0.8 fusion.54
  108.3 1.3 reshape.102
  109.6 1.9 copy.134
  111.5 5.4 %all-to-all-start.7 = ((bf16[6,192,128]{2,0,1:T(8,128)(2,1)}), bf16[6,192,128]{2,0,1:T(8,128)(2,1)S(1)}, u32[]{:S(2)}, u32[]{:S(2)}) async-start(bf16[6,192,128]{2,0,1:T(8,128)(2,1)} %copy.134), calls=%async_computation.7 | async-start | bytes 786432 | tf_op jit(solution)/shard_map/all_to_all | solution.py:120
  116.9 1.0 copy.126
  117.9 17.4 %all-to-all-done.7 = bf16[6,192,128]{2,0,1:T(8,128)(2,1)S(1)} async-done(((bf16[6,192,128]{2,0,1:T(8,128)(2,1)}), bf16[6,192,128]{2,0,1:T(8,128)(2,1)S(1)}, u32[]{:S(2)}, u32[]{:S(2)}) %all-to-all-start.7) | async-done | bytes 294944 | tf_op jit(solution)/shard_map/all_to_all | solution.py:120
  135.3 3.5 %all-to-all-start.5 = ((bf16[6,192,128]{2,0,1:T(8,128)(2,1)}), bf16[6,192,128]{2,0,1:T(8,128)(2,1)S(1)}, u32[]{:S(2)}, u32[]{:S(2)}) async-start(bf16[6,192,128]{2,0,1:T(8,128)(2,1)} %copy.126), calls=%async_computation.5 | async-start | bytes 786432 | tf_op jit(solution)/shard_map/all_to_all | solution.py:114
  138.8 1.9 copy.130
  140.7 6.9 %all-to-all-done.5 = bf16[6,192,128]{2,0,1:T(8,128)(2,1)S(1)} async-done(((bf16[6,192,128]{2,0,1:T(8,128)(2,1)}), bf16[6,192,128]{2,0,1:T(8,128)(2,1)S(1)}, u32[]{:S(2)}, u32[]{:S(2)}) %all-to-all-start.5) | async-done | bytes 294944 | tf_op jit(solution)/shard_map/all_to_all | solution.py:114
  147.6 3.5 %all-to-all-start.6 = ((bf16[6,192,128]{2,0,1:T(8,128)(2,1)}), bf16[6,192,128]{2,0,1:T(8,128)(2,1)S(1)}, u32[]{:S(2)}, u32[]{:S(2)}) async-start(bf16[6,192,128]{2,0,1:T(8,128)(2,1)} %copy.130), calls=%async_computation.6 | async-start | bytes 786432 | tf_op jit(solution)/shard_map/all_to_all | solution.py:117
  151.2 1.1 reshape.103
  152.2 0.9 copy.146
  153.2 0.8 copy.136
  154.7 5.2 %all-to-all-done.6 = bf16[6,192,128]{2,0,1:T(8,128)(2,1)S(1)} async-done(((bf16[6,192,128]{2,0,1:T(8,128)(2,1)}), bf16[6,192,128]{2,0,1:T(8,128)(2,1)S(1)}, u32[]{:S(2)}, u32[]{:S(2)}) %all-to-all-start.6) | async-done | bytes 294944 | tf_op jit(solution)/shard_map/all_to_all | solution.py:117
  160.0 0.8 copy.132
  160.7 29.2 %reduce-scatter.5.cloned.1.call-done = f32[4,48,24]{1,2,0:T(8,128)} async-done(((f32[4,48,192]{1,2,0:T(8,128)}), f32[4,48,24]{1,2,0:T(8,128)}) %reduce-scatter.5.cloned.1.call-update) | async-done | bytes 18448 | tf_op jit(solution)/shard_map/reduce_scatter | solution.py:125
  (143 shorter events, 18.5 us)
Async XLA Ops:
  7.2 51.3 %copy-start.10 = (bf16[4,48,24]{1,2,0:T(8,128)(2,1)S(1)}, bf16[4,48,24]{1,2,0:T(8,128)(2,1)}, u32[]{:S(2)}) copy-start(bf16[4,48,24]{1,2,0:T(8,128)(2,1)} %param.11) | copy-start | bytes 27652
  54.9 29.4 %all-to-all-start.3 = ((bf16[24,48,128]{2,1,0:T(8,128)(2,1)}), bf16[24,48,128]{2,1,0:T(8,128)(2,1)S(1)}, u32[]{:S(2)}, u32[]{:S(2)}) async-start(bf16[24,48,128]{2,1,0:T(8,128)(2,1)} %param.13), calls=%async_computation.3 | async-start | bytes 589824 | tf_op jit(solution)/shard_map/all_to_all | solution.py:106
  58.4 92.8 %reduce-scatter.7.cloned.1.call-start = ((), (), s32[]{:S(2)}) async-start(), calls=%async_computation.11 | async-start | bytes 737280
  84.4 2.3 %copy-start = (bf16[4,192,192]{1,2,0:T(8,128)(2,1)}, bf16[4,192,192]{1,2,0:T(8,128)(2,1)S(1)}, u32[]{:S(2)}) copy-start(bf16[4,192,192]{1,2,0:T(8,128)(2,1)S(1)} %get-tuple-element.381) | copy-start | bytes 884740 | tf_op jit(solution)/shard_map/while
  84.4 2.3 %copy-start.3 = (bf16[3,2,192,128]{3,2,1,0:T(8,128)(2,1)}, bf16[3,2,192,128]{3,2,1,0:T(8,128)(2,1)S(1)}, u32[]{:S(2)}) copy-start(bf16[3,2,192,128]{3,2,1,0:T(8,128)(2,1)S(1)} %get-tuple-element.380) | copy-start | bytes 884740 | tf_op jit(solution)/shard_map/while
  84.4 2.3 %copy-start.5 = (bf16[3,2,192,128]{3,2,1,0:T(8,128)(2,1)}, bf16[3,2,192,128]{3,2,1,0:T(8,128)(2,1)S(1)}, u32[]{:S(2)}) copy-start(bf16[3,2,192,128]{3,2,1,0:T(8,128)(2,1)S(1)} %get-tuple-element.384) | copy-start | bytes 884740 | tf_op jit(solution)/shard_map/while
  84.4 2.3 %copy-start.7 = (bf16[3,2,192,128]{3,2,1,0:T(8,128)(2,1)}, bf16[3,2,192,128]{3,2,1,0:T(8,128)(2,1)S(1)}, u32[]{:S(2)}) copy-start(bf16[3,2,192,128]{3,2,1,0:T(8,128)(2,1)S(1)} %get-tuple-element.383) | copy-start | bytes 884740 | tf_op jit(solution)/shard_map/while
  90.0 2.2 %copy-start.1 = (bf16[4,192,192]{1,2,0:T(8,128)(2,1)S(1)}, bf16[4,192,192]{1,2,0:T(8,128)(2,1)}, u32[]{:S(2)}) copy-start(bf16[4,192,192]{1,2,0:T(8,128)(2,1)} %copy-done) | copy-start | bytes 884740 | tf_op jit(solution)/shard_map/while
  90.0 2.2 %copy-start.4 = (bf16[3,2,192,128]{3,2,1,0:T(8,128)(2,1)S(1)}, bf16[3,2,192,128]{3,2,1,0:T(8,128)(2,1)}, u32[]{:S(2)}) copy-start(bf16[3,2,192,128]{3,2,1,0:T(8,128)(2,1)} %copy-done.3) | copy-start | bytes 884740 | tf_op jit(solution)/shard_map/while
  90.0 2.2 %copy-start.6 = (bf16[3,2,192,128]{3,2,1,0:T(8,128)(2,1)S(1)}, bf16[3,2,192,128]{3,2,1,0:T(8,128)(2,1)}, u32[]{:S(2)}) copy-start(bf16[3,2,192,128]{3,2,1,0:T(8,128)(2,1)} %copy-done.5) | copy-start | bytes 884740 | tf_op jit(solution)/shard_map/while
  90.0 2.2 %copy-start.8 = (bf16[3,2,192,128]{3,2,1,0:T(8,128)(2,1)S(1)}, bf16[3,2,192,128]{3,2,1,0:T(8,128)(2,1)}, u32[]{:S(2)}) copy-start(bf16[3,2,192,128]{3,2,1,0:T(8,128)(2,1)} %copy-done.7) | copy-start | bytes 884740 | tf_op jit(solution)/shard_map/while
  92.2 2.3 %copy-start = (bf16[4,192,192]{1,2,0:T(8,128)(2,1)}, bf16[4,192,192]{1,2,0:T(8,128)(2,1)S(1)}, u32[]{:S(2)}) copy-start(bf16[4,192,192]{1,2,0:T(8,128)(2,1)S(1)} %get-tuple-element.381) | copy-start | bytes 884740 | tf_op jit(solution)/shard_map/while
  92.3 2.3 %copy-start.3 = (bf16[3,2,192,128]{3,2,1,0:T(8,128)(2,1)}, bf16[3,2,192,128]{3,2,1,0:T(8,128)(2,1)S(1)}, u32[]{:S(2)}) copy-start(bf16[3,2,192,128]{3,2,1,0:T(8,128)(2,1)S(1)} %get-tuple-element.380) | copy-start | bytes 884740 | tf_op jit(solution)/shard_map/while
  92.3 2.3 %copy-start.5 = (bf16[3,2,192,128]{3,2,1,0:T(8,128)(2,1)}, bf16[3,2,192,128]{3,2,1,0:T(8,128)(2,1)S(1)}, u32[]{:S(2)}) copy-start(bf16[3,2,192,128]{3,2,1,0:T(8,128)(2,1)S(1)} %get-tuple-element.384) | copy-start | bytes 884740 | tf_op jit(solution)/shard_map/while
  92.3 2.3 %copy-start.7 = (bf16[3,2,192,128]{3,2,1,0:T(8,128)(2,1)}, bf16[3,2,192,128]{3,2,1,0:T(8,128)(2,1)S(1)}, u32[]{:S(2)}) copy-start(bf16[3,2,192,128]{3,2,1,0:T(8,128)(2,1)S(1)} %get-tuple-element.383) | copy-start | bytes 884740 | tf_op jit(solution)/shard_map/while
  97.8 2.2 %copy-start.1 = (bf16[4,192,192]{1,2,0:T(8,128)(2,1)S(1)}, bf16[4,192,192]{1,2,0:T(8,128)(2,1)}, u32[]{:S(2)}) copy-start(bf16[4,192,192]{1,2,0:T(8,128)(2,1)} %copy-done) | copy-start | bytes 884740 | tf_op jit(solution)/shard_map/while
  97.8 2.2 %copy-start.4 = (bf16[3,2,192,128]{3,2,1,0:T(8,128)(2,1)S(1)}, bf16[3,2,192,128]{3,2,1,0:T(8,128)(2,1)}, u32[]{:S(2)}) copy-start(bf16[3,2,192,128]{3,2,1,0:T(8,128)(2,1)} %copy-done.3) | copy-start | bytes 884740 | tf_op jit(solution)/shard_map/while
  97.8 2.2 %copy-start.6 = (bf16[3,2,192,128]{3,2,1,0:T(8,128)(2,1)S(1)}, bf16[3,2,192,128]{3,2,1,0:T(8,128)(2,1)}, u32[]{:S(2)}) copy-start(bf16[3,2,192,128]{3,2,1,0:T(8,128)(2,1)} %copy-done.5) | copy-start | bytes 884740 | tf_op jit(solution)/shard_map/while
  97.8 2.2 %copy-start.8 = (bf16[3,2,192,128]{3,2,1,0:T(8,128)(2,1)S(1)}, bf16[3,2,192,128]{3,2,1,0:T(8,128)(2,1)}, u32[]{:S(2)}) copy-start(bf16[3,2,192,128]{3,2,1,0:T(8,128)(2,1)} %copy-done.7) | copy-start | bytes 884740 | tf_op jit(solution)/shard_map/while
  100.1 2.3 %copy-start = (bf16[4,192,192]{1,2,0:T(8,128)(2,1)}, bf16[4,192,192]{1,2,0:T(8,128)(2,1)S(1)}, u32[]{:S(2)}) copy-start(bf16[4,192,192]{1,2,0:T(8,128)(2,1)S(1)} %get-tuple-element.381) | copy-start | bytes 884740 | tf_op jit(solution)/shard_map/while
  100.1 2.3 %copy-start.3 = (bf16[3,2,192,128]{3,2,1,0:T(8,128)(2,1)}, bf16[3,2,192,128]{3,2,1,0:T(8,128)(2,1)S(1)}, u32[]{:S(2)}) copy-start(bf16[3,2,192,128]{3,2,1,0:T(8,128)(2,1)S(1)} %get-tuple-element.380) | copy-start | bytes 884740 | tf_op jit(solution)/shard_map/while
  100.1 2.3 %copy-start.5 = (bf16[3,2,192,128]{3,2,1,0:T(8,128)(2,1)}, bf16[3,2,192,128]{3,2,1,0:T(8,128)(2,1)S(1)}, u32[]{:S(2)}) copy-start(bf16[3,2,192,128]{3,2,1,0:T(8,128)(2,1)S(1)} %get-tuple-element.384) | copy-start | bytes 884740 | tf_op jit(solution)/shard_map/while
  100.1 2.3 %copy-start.7 = (bf16[3,2,192,128]{3,2,1,0:T(8,128)(2,1)}, bf16[3,2,192,128]{3,2,1,0:T(8,128)(2,1)S(1)}, u32[]{:S(2)}) copy-start(bf16[3,2,192,128]{3,2,1,0:T(8,128)(2,1)S(1)} %get-tuple-element.383) | copy-start | bytes 884740 | tf_op jit(solution)/shard_map/while
  105.6 2.2 %copy-start.1 = (bf16[4,192,192]{1,2,0:T(8,128)(2,1)S(1)}, bf16[4,192,192]{1,2,0:T(8,128)(2,1)}, u32[]{:S(2)}) copy-start(bf16[4,192,192]{1,2,0:T(8,128)(2,1)} %copy-done) | copy-start | bytes 884740 | tf_op jit(solution)/shard_map/while
  105.7 2.2 %copy-start.4 = (bf16[3,2,192,128]{3,2,1,0:T(8,128)(2,1)S(1)}, bf16[3,2,192,128]{3,2,1,0:T(8,128)(2,1)}, u32[]{:S(2)}) copy-start(bf16[3,2,192,128]{3,2,1,0:T(8,128)(2,1)} %copy-done.3) | copy-start | bytes 884740 | tf_op jit(solution)/shard_map/while
  105.7 2.2 %copy-start.6 = (bf16[3,2,192,128]{3,2,1,0:T(8,128)(2,1)S(1)}, bf16[3,2,192,128]{3,2,1,0:T(8,128)(2,1)}, u32[]{:S(2)}) copy-start(bf16[3,2,192,128]{3,2,1,0:T(8,128)(2,1)} %copy-done.5) | copy-start | bytes 884740 | tf_op jit(solution)/shard_map/while
  105.7 2.2 %copy-start.8 = (bf16[3,2,192,128]{3,2,1,0:T(8,128)(2,1)S(1)}, bf16[3,2,192,128]{3,2,1,0:T(8,128)(2,1)}, u32[]{:S(2)}) copy-start(bf16[3,2,192,128]{3,2,1,0:T(8,128)(2,1)} %copy-done.7) | copy-start | bytes 884740 | tf_op jit(solution)/shard_map/while
  108.3 8.6 %copy-start.9 = (bf16[3,2,192,128]{3,2,1,0:T(8,128)(2,1)S(1)}, bf16[3,2,192,128]{3,2,1,0:T(8,128)(2,1)}, u32[]{:S(2)}) copy-start(bf16[3,2,192,128]{3,2,1,0:T(8,128)(2,1)} %get-tuple-element.144) | copy-start | bytes 884740
  111.5 23.8 %all-to-all-start.7 = ((bf16[6,192,128]{2,0,1:T(8,128)(2,1)}), bf16[6,192,128]{2,0,1:T(8,128)(2,1)S(1)}, u32[]{:S(2)}, u32[]{:S(2)}) async-start(bf16[6,192,128]{2,0,1:T(8,128)(2,1)} %copy.134), calls=%async_computation.7 | async-start | bytes 786432 | tf_op jit(solution)/shard_map/all_to_all | solution.py:120
  135.3 12.3 %all-to-all-start.5 = ((bf16[6,192,128]{2,0,1:T(8,128)(2,1)}), bf16[6,192,128]{2,0,1:T(8,128)(2,1)S(1)}, u32[]{:S(2)}, u32[]{:S(2)}) async-start(bf16[6,192,128]{2,0,1:T(8,128)(2,1)} %copy.126), calls=%async_computation.5 | async-start | bytes 786432 | tf_op jit(solution)/shard_map/all_to_all | solution.py:114
  147.6 12.3 %all-to-all-start.6 = ((bf16[6,192,128]{2,0,1:T(8,128)(2,1)}), bf16[6,192,128]{2,0,1:T(8,128)(2,1)S(1)}, u32[]{:S(2)}, u32[]{:S(2)}) async-start(bf16[6,192,128]{2,0,1:T(8,128)(2,1)} %copy.130), calls=%async_computation.6 | async-start | bytes 786432 | tf_op jit(solution)/shard_map/all_to_all | solution.py:117
  151.1 38.8 %reduce-scatter.5.cloned.1.call-start = ((), (), s32[]{:S(2)}) async-start(), calls=%async_computation.10 | async-start | bytes 442368 | tf_op jit(solution)/shard_map/reduce_scatter | solution.py:125
  (3 other events, 2.7 us)
Sparse Core Ops, SparseCore 0:
  109.7 25.3 reduce-scatter.6
  155.6 34.3 reduce-scatter.4
where the time goes:
time: 198 us; the launch traced here: 197 us
  blocking collectives  71.3 us (36%)
  waiting for transfers between devices  58.9 us (30%)
  local copies, waits for them, and re-layouts  26.4 us (13%)
  starting transfers between devices  15.8 us (8%)
  between operations  14.2 us (7%)
  matrix products  7.33 us (4%)
  other arithmetic  2.1 us (1%)
    reduce_scatter x1, waiting for transfers between devices, local(): lax.psum_scatter(bias_part, 'row', scatter_dimension=2, tiled=True)  29.2 us
    all_to_all x1, waiting for transfers between devices, local(): lax.all_to_all(grad_values.astype(jnp.bfloat16), 'col', split_axis=1, con...  17.4 us
    all_gather x1, blocking collectives, local(): bias_full = lax.all_gather(bias_rows, 'col', axis=1, tiled=True)  15.1 us
    all_to_all x1, blocking collectives, local(): lax.all_to_all(query_proj, 'col', split_axis=0, concat_axis=1, tiled=True)  11.8 us
    all_to_all x1, blocking collectives, local(): lax.all_to_all(key_proj, 'col', split_axis=0, concat_axis=1, tiled=True)  11.7 us
    all_to_all x1, blocking collectives, local(): lax.all_to_all(mask_low, 'col', split_axis=0, concat_axis=1, tiled=True)  11.7 us
    all_to_all x1, blocking collectives, local(): lax.all_to_all(value_proj, 'col', split_axis=0, concat_axis=1, tiled=True)  11.6 us
    all_gather x1, blocking collectives, local(): bias_rows = lax.all_gather(pair_bias, 'row', axis=2, tiled=True)  9.27 us
  transfers between devices with their start and end apart: 6, of which 4 were waited for; matrix products, arithmetic and copies ran while one was open for 5% of the time, Pallas kernels for 0%

commit v1 on v0

--- a/solution.py
+++ b/solution.py
@@ -6,6 +6,12 @@
 
 HEADS = 4
 HEAD_DIM = 32
+
+
+def stacked_exchange(x, axis, split, join):
+    cells = jnp.split(x, lax.axis_size(axis), axis=split)
+    arrived = lax.all_to_all(jnp.stack(cells), axis, 0, 0)
+    return jnp.concatenate(arrived, axis=join)
 
 
 def block_grads(queries, keys_all, values_all, grads, mask_all, bias_full):
@@ -104,7 +110,7 @@
         lax.all_to_all(key_proj, "col", split_axis=0, concat_axis=1, tiled=True),
         lax.all_to_all(value_proj, "col", split_axis=0, concat_axis=1, tiled=True),
         lax.all_to_all(grad_out, "col", split_axis=0, concat_axis=1, tiled=True),
-        lax.all_to_all(mask_low, "col", split_axis=0, concat_axis=1, tiled=True),
+        stacked_exchange(mask_low, "col", 0, 1),
     )
     bias_full = lax.all_gather(bias_rows, "col", axis=1, tiled=True)
     grad_queries, grad_keys, grad_values, bias_whole = all_blocks(

time: 198 us -> 198 us (level)
  no operation moved by 1% of the time
where the time goes in v1:
time: 198 us; the launch traced here: 197 us
  blocking collectives  71.3 us (36%)
  waiting for transfers between devices  58.9 us (30%)
  local copies, waits for them, and re-layouts  26.5 us (13%)
  starting transfers between devices  15.8 us (8%)
  between operations  14.2 us (7%)
  matrix products  7.32 us (4%)
  other arithmetic  2.11 us (1%)
    reduce_scatter x1, waiting for transfers between devices, local(): lax.psum_scatter(bias_part, 'row', scatter_dimension=2, tiled=True)  29.2 us
    all_to_all x1, waiting for transfers between devices, local(): lax.all_to_all(grad_values.astype(jnp.bfloat16), 'col', split_axis=1, con...  17.4 us
    all_gather x1, blocking collectives, local(): bias_full = lax.all_gather(bias_rows, 'col', axis=1, tiled=True)  15.1 us
    all_to_all x1, blocking collectives, local(): lax.all_to_all(query_proj, 'col', split_axis=0, concat_axis=1, tiled=True)  11.8 us
    all_to_all x1, blocking collectives, local(): lax.all_to_all(key_proj, 'col', split_axis=0, concat_axis=1, tiled=True)  11.7 us
    all_to_all x1, blocking collectives, stacked_exchange(): arrived = lax.all_to_all(jnp.stack(cells), axis, 0, 0)  11.7 us
    all_to_all x1, blocking collectives, local(): lax.all_to_all(value_proj, 'col', split_axis=0, concat_axis=1, tiled=True)  11.6 us
    all_gather x1, blocking collectives, local(): bias_rows = lax.all_gather(pair_bias, 'row', axis=2, tiled=True)  9.27 us
  transfers between devices with their start and end apart: 6, of which 4 were waited for; matrix products, arithmetic and copies ran while one was open for 5% of the time, Pallas kernels for 0%

profile of v1, /device:TPU:0, one launch (start us, length us, event | category | flops | bytes accessed | tf_op | source)
XLA Modules:
  0.0 196.9 jit_solution(5455818766581730597)
XLA Ops:
  8.0 11.7 %all_to_all.119 = bf16[4,2,144]{2,1,0:T(2,128)(2,1)S(1)} all-to-all(bf16[4,2,144]{2,1,0:T(2,128)(2,1)S(1)} %reshape.100), channel_id=1, replica_groups=mesh['row'=8,'col'=4] {'col'}, dimensions={0} | all-to-all | bytes 4608 | tf_op jit(solution)/shard_map/all_to_all | solution.py:13
  19.7 11.8 %all_to_all.120 = bf16[24,48,128]{2,1,0:T(8,128)(2,1)S(1)} all-to-all(bf16[24,48,128]{2,1,0:T(8,128)(2,1)} %param.8), channel_id=1, replica_groups=mesh['row'=8,'col'=4] {'col'}, dimensions={0} | all-to-all | bytes 589824 | tf_op jit(solution)/shard_map/all_to_all | solution.py:109
  31.6 11.7 %all_to_all.121 = bf16[24,48,128]{2,1,0:T(8,128)(2,1)S(1)} all-to-all(bf16[24,48,128]{2,1,0:T(8,128)(2,1)} %param.9), channel_id=1, replica_groups=mesh['row'=8,'col'=4] {'col'}, dimensions={0} | all-to-all | bytes 589824 | tf_op jit(solution)/shard_map/all_to_all | solution.py:110
  43.3 11.6 %all_to_all.122 = bf16[24,48,128]{2,1,0:T(8,128)(2,1)S(1)} all-to-all(bf16[24,48,128]{2,1,0:T(8,128)(2,1)} %param.10), channel_id=1, replica_groups=mesh['row'=8,'col'=4] {'col'}, dimensions={0} | all-to-all | bytes 589824 | tf_op jit(solution)/shard_map/all_to_all | solution.py:111
  54.9 3.5 %all-to-all-start.3 = ((bf16[24,48,128]{2,1,0:T(8,128)(2,1)}), bf16[24,48,128]{2,1,0:T(8,128)(2,1)S(1)}, u32[]{:S(2)}, u32[]{:S(2)}) async-start(bf16[24,48,128]{2,1,0:T(8,128)(2,1)} %param.13), calls=%async_computation.3 | async-start | bytes 589824 | tf_op jit(solution)/shard_map/all_to_all | solution.py:112
  58.5 9.3 %all_gather.6 = bf16[4,48,192]{1,0,2:T(4,128)(2,1)S(1)} all-gather(bf16[4,48,24]{1,0,2:T(4,128)(2,1)S(1)} %copy.116), channel_id=1, replica_groups=mesh['row'=8,'col'=4] {'row'}, dimensions={2}, use_global_device_ids=true | all-gather | bytes 82944 | tf_op jit(solution)/shard_map/all_gather | solution.py:106
  68.0 15.1 %all_gather.7 = bf16[4,192,192]{2,0,1:T(4,128)(2,1)S(1)} all-gather(bf16[4,48,192]{2,0,1:T(4,128)(2,1)S(1)} %copy.117), channel_id=1, replica_groups=mesh['row'=8,'col'=4] {'col'}, dimensions={1}, use_global_device_ids=true | all-gather | bytes 368640 | tf_op jit(solution)/shard_map/all_gather | solution.py:115
  84.4 23.6 %while.19 = (s32[]{:T(128)}, f32[4,192,192]{1,2,0:T(8,128)S(1)}, bf16[3,2,192,128]{3,2,1,0:T(8,128)(2,1)}, bf16[3,2,192,128]{3,2,1,0:T(8,128)(2,1)}, bf16[3,2,19...) while((s32[]{:T(128)}, f32[4,192,192]{1,2,0:T(8,128)S(1)}, ...), condition=%wide.region_5.6_spmd.clone, body=%wide.region_0.5_spmd.clone.sunk | while | flops 117423936 | bytes 24709288 | solution.py:86
  84.5 1.0 copy.165
  85.7 0.9 constant_dynamic-slice_fusion.10
  86.9 0.8 fusion.54
  92.4 1.0 copy.165
  93.6 0.9 constant_dynamic-slice_fusion.10
  94.7 0.8 fusion.54
  100.2 1.0 copy.165
  101.4 0.9 constant_dynamic-slice_fusion.10
  102.6 0.8 fusion.54
  108.4 1.3 reshape.98
  109.7 1.9 copy.135
  111.6 5.4 %all-to-all-start.7 = ((bf16[6,192,128]{2,0,1:T(8,128)(2,1)}), bf16[6,192,128]{2,0,1:T(8,128)(2,1)S(1)}, u32[]{:S(2)}, u32[]{:S(2)}) async-start(bf16[6,192,128]{2,0,1:T(8,128)(2,1)} %copy.135), calls=%async_computation.7 | async-start | bytes 786432 | tf_op jit(solution)/shard_map/all_to_all | solution.py:126
  117.0 1.0 copy.127
  118.0 17.4 %all-to-all-done.7 = bf16[6,192,128]{2,0,1:T(8,128)(2,1)S(1)} async-done(((bf16[6,192,128]{2,0,1:T(8,128)(2,1)}), bf16[6,192,128]{2,0,1:T(8,128)(2,1)S(1)}, u32[]{:S(2)}, u32[]{:S(2)}) %all-to-all-start.7) | async-done | bytes 294944 | tf_op jit(solution)/shard_map/all_to_all | solution.py:126
  135.4 3.5 %all-to-all-start.5 = ((bf16[6,192,128]{2,0,1:T(8,128)(2,1)}), bf16[6,192,128]{2,0,1:T(8,128)(2,1)S(1)}, u32[]{:S(2)}, u32[]{:S(2)}) async-start(bf16[6,192,128]{2,0,1:T(8,128)(2,1)} %copy.127), calls=%async_computation.5 | async-start | bytes 786432 | tf_op jit(solution)/shard_map/all_to_all | solution.py:120
  138.9 1.9 copy.131
  140.8 6.9 %all-to-all-done.5 = bf16[6,192,128]{2,0,1:T(8,128)(2,1)S(1)} async-done(((bf16[6,192,128]{2,0,1:T(8,128)(2,1)}), bf16[6,192,128]{2,0,1:T(8,128)(2,1)S(1)}, u32[]{:S(2)}, u32[]{:S(2)}) %all-to-all-start.5) | async-done | bytes 294944 | tf_op jit(solution)/shard_map/all_to_all | solution.py:120
  147.7 3.5 %all-to-all-start.6 = ((bf16[6,192,128]{2,0,1:T(8,128)(2,1)}), bf16[6,192,128]{2,0,1:T(8,128)(2,1)S(1)}, u32[]{:S(2)}, u32[]{:S(2)}) async-start(bf16[6,192,128]{2,0,1:T(8,128)(2,1)} %copy.131), calls=%async_computation.6 | async-start | bytes 786432 | tf_op jit(solution)/shard_map/all_to_all | solution.py:123
  151.3 1.1 reshape.99
  152.3 0.9 copy.147
  153.3 0.8 copy.137
  154.8 5.2 %all-to-all-done.6 = bf16[6,192,128]{2,0,1:T(8,128)(2,1)S(1)} async-done(((bf16[6,192,128]{2,0,1:T(8,128)(2,1)}), bf16[6,192,128]{2,0,1:T(8,128)(2,1)S(1)}, u32[]{:S(2)}, u32[]{:S(2)}) %all-to-all-start.6) | async-done | bytes 294944 | tf_op jit(solution)/shard_map/all_to_all | solution.py:123
  160.0 0.8 copy.133
  160.8 29.2 %reduce-scatter.5.cloned.1.call-done = f32[4,48,24]{1,2,0:T(8,128)} async-done(((f32[4,48,192]{1,2,0:T(8,128)}), f32[4,48,24]{1,2,0:T(8,128)}) %reduce-scatter.5.cloned.1.call-update) | async-done | bytes 18448 | tf_op jit(solution)/shard_map/reduce_scatter | solution.py:131
  (144 shorter events, 18.6 us)
Async XLA Ops:
  7.2 51.3 %copy-start.10 = (bf16[4,48,24]{1,2,0:T(8,128)(2,1)S(1)}, bf16[4,48,24]{1,2,0:T(8,128)(2,1)}, u32[]{:S(2)}) copy-start(bf16[4,48,24]{1,2,0:T(8,128)(2,1)} %param.11) | copy-start | bytes 27652
  54.9 29.4 %all-to-all-start.3 = ((bf16[24,48,128]{2,1,0:T(8,128)(2,1)}), bf16[24,48,128]{2,1,0:T(8,128)(2,1)S(1)}, u32[]{:S(2)}, u32[]{:S(2)}) async-start(bf16[24,48,128]{2,1,0:T(8,128)(2,1)} %param.13), calls=%async_computation.3 | async-start | bytes 589824 | tf_op jit(solution)/shard_map/all_to_all | solution.py:112
  58.4 92.9 %reduce-scatter.7.cloned.1.call-start = ((), (), s32[]{:S(2)}) async-start(), calls=%async_computation.11 | async-start | bytes 737280
  84.4 2.3 %copy-start = (bf16[4,192,192]{1,2,0:T(8,128)(2,1)}, bf16[4,192,192]{1,2,0:T(8,128)(2,1)S(1)}, u32[]{:S(2)}) copy-start(bf16[4,192,192]{1,2,0:T(8,128)(2,1)S(1)} %get-tuple-element.385) | copy-start | bytes 884740 | tf_op jit(solution)/shard_map/while
  84.4 2.3 %copy-start.3 = (bf16[3,2,192,128]{3,2,1,0:T(8,128)(2,1)}, bf16[3,2,192,128]{3,2,1,0:T(8,128)(2,1)S(1)}, u32[]{:S(2)}) copy-start(bf16[3,2,192,128]{3,2,1,0:T(8,128)(2,1)S(1)} %get-tuple-element.384) | copy-start | bytes 884740 | tf_op jit(solution)/shard_map/while
  84.5 2.3 %copy-start.5 = (bf16[3,2,192,128]{3,2,1,0:T(8,128)(2,1)}, bf16[3,2,192,128]{3,2,1,0:T(8,128)(2,1)S(1)}, u32[]{:S(2)}) copy-start(bf16[3,2,192,128]{3,2,1,0:T(8,128)(2,1)S(1)} %get-tuple-element.388) | copy-start | bytes 884740 | tf_op jit(solution)/shard_map/while
  84.5 2.3 %copy-start.7 = (bf16[3,2,192,128]{3,2,1,0:T(8,128)(2,1)}, bf16[3,2,192,128]{3,2,1,0:T(8,128)(2,1)S(1)}, u32[]{:S(2)}) copy-start(bf16[3,2,192,128]{3,2,1,0:T(8,128)(2,1)S(1)} %get-tuple-element.387) | copy-start | bytes 884740 | tf_op jit(solution)/shard_map/while
  90.0 2.2 %copy-start.1 = (bf16[4,192,192]{1,2,0:T(8,128)(2,1)S(1)}, bf16[4,192,192]{1,2,0:T(8,128)(2,1)}, u32[]{:S(2)}) copy-start(bf16[4,192,192]{1,2,0:T(8,128)(2,1)} %copy-done) | copy-start | bytes 884740 | tf_op jit(solution)/shard_map/while
  90.0 2.2 %copy-start.4 = (bf16[3,2,192,128]{3,2,1,0:T(8,128)(2,1)S(1)}, bf16[3,2,192,128]{3,2,1,0:T(8,128)(2,1)}, u32[]{:S(2)}) copy-start(bf16[3,2,192,128]{3,2,1,0:T(8,128)(2,1)} %copy-done.3) | copy-start | bytes 884740 | tf_op jit(solution)/shard_map/while
  90.0 2.2 %copy-start.6 = (bf16[3,2,192,128]{3,2,1,0:T(8,128)(2,1)S(1)}, bf16[3,2,192,128]{3,2,1,0:T(8,128)(2,1)}, u32[]{:S(2)}) copy-start(bf16[3,2,192,128]{3,2,1,0:T(8,128)(2,1)} %copy-done.5) | copy-start | bytes 884740 | tf_op jit(solution)/shard_map/while
  90.0 2.2 %copy-start.8 = (bf16[3,2,192,128]{3,2,1,0:T(8,128)(2,1)S(1)}, bf16[3,2,192,128]{3,2,1,0:T(8,128)(2,1)}, u32[]{:S(2)}) copy-start(bf16[3,2,192,128]{3,2,1,0:T(8,128)(2,1)} %copy-done.7) | copy-start | bytes 884740 | tf_op jit(solution)/shard_map/while
  92.3 2.3 %copy-start = (bf16[4,192,192]{1,2,0:T(8,128)(2,1)}, bf16[4,192,192]{1,2,0:T(8,128)(2,1)S(1)}, u32[]{:S(2)}) copy-start(bf16[4,192,192]{1,2,0:T(8,128)(2,1)S(1)} %get-tuple-element.385) | copy-start | bytes 884740 | tf_op jit(solution)/shard_map/while
  92.3 2.3 %copy-start.3 = (bf16[3,2,192,128]{3,2,1,0:T(8,128)(2,1)}, bf16[3,2,192,128]{3,2,1,0:T(8,128)(2,1)S(1)}, u32[]{:S(2)}) copy-start(bf16[3,2,192,128]{3,2,1,0:T(8,128)(2,1)S(1)} %get-tuple-element.384) | copy-start | bytes 884740 | tf_op jit(solution)/shard_map/while
  92.3 2.3 %copy-start.5 = (bf16[3,2,192,128]{3,2,1,0:T(8,128)(2,1)}, bf16[3,2,192,128]{3,2,1,0:T(8,128)(2,1)S(1)}, u32[]{:S(2)}) copy-start(bf16[3,2,192,128]{3,2,1,0:T(8,128)(2,1)S(1)} %get-tuple-element.388) | copy-start | bytes 884740 | tf_op jit(solution)/shard_map/while
  92.3 2.3 %copy-start.7 = (bf16[3,2,192,128]{3,2,1,0:T(8,128)(2,1)}, bf16[3,2,192,128]{3,2,1,0:T(8,128)(2,1)S(1)}, u32[]{:S(2)}) copy-start(bf16[3,2,192,128]{3,2,1,0:T(8,128)(2,1)S(1)} %get-tuple-element.387) | copy-start | bytes 884740 | tf_op jit(solution)/shard_map/while
  97.9 2.2 %copy-start.1 = (bf16[4,192,192]{1,2,0:T(8,128)(2,1)S(1)}, bf16[4,192,192]{1,2,0:T(8,128)(2,1)}, u32[]{:S(2)}) copy-start(bf16[4,192,192]{1,2,0:T(8,128)(2,1)} %copy-done) | copy-start | bytes 884740 | tf_op jit(solution)/shard_map/while
  97.9 2.2 %copy-start.4 = (bf16[3,2,192,128]{3,2,1,0:T(8,128)(2,1)S(1)}, bf16[3,2,192,128]{3,2,1,0:T(8,128)(2,1)}, u32[]{:S(2)}) copy-start(bf16[3,2,192,128]{3,2,1,0:T(8,128)(2,1)} %copy-done.3) | copy-start | bytes 884740 | tf_op jit(solution)/shard_map/while
  97.9 2.2 %copy-start.6 = (bf16[3,2,192,128]{3,2,1,0:T(8,128)(2,1)S(1)}, bf16[3,2,192,128]{3,2,1,0:T(8,128)(2,1)}, u32[]{:S(2)}) copy-start(bf16[3,2,192,128]{3,2,1,0:T(8,128)(2,1)} %copy-done.5) | copy-start | bytes 884740 | tf_op jit(solution)/shard_map/while
  97.9 2.2 %copy-start.8 = (bf16[3,2,192,128]{3,2,1,0:T(8,128)(2,1)S(1)}, bf16[3,2,192,128]{3,2,1,0:T(8,128)(2,1)}, u32[]{:S(2)}) copy-start(bf16[3,2,192,128]{3,2,1,0:T(8,128)(2,1)} %copy-done.7) | copy-start | bytes 884740 | tf_op jit(solution)/shard_map/while
  100.1 2.3 %copy-start = (bf16[4,192,192]{1,2,0:T(8,128)(2,1)}, bf16[4,192,192]{1,2,0:T(8,128)(2,1)S(1)}, u32[]{:S(2)}) copy-start(bf16[4,192,192]{1,2,0:T(8,128)(2,1)S(1)} %get-tuple-element.385) | copy-start | bytes 884740 | tf_op jit(solution)/shard_map/while
  100.1 2.3 %copy-start.3 = (bf16[3,2,192,128]{3,2,1,0:T(8,128)(2,1)}, bf16[3,2,192,128]{3,2,1,0:T(8,128)(2,1)S(1)}, u32[]{:S(2)}) copy-start(bf16[3,2,192,128]{3,2,1,0:T(8,128)(2,1)S(1)} %get-tuple-element.384) | copy-start | bytes 884740 | tf_op jit(solution)/shard_map/while
  100.2 2.3 %copy-start.5 = (bf16[3,2,192,128]{3,2,1,0:T(8,128)(2,1)}, bf16[3,2,192,128]{3,2,1,0:T(8,128)(2,1)S(1)}, u32[]{:S(2)}) copy-start(bf16[3,2,192,128]{3,2,1,0:T(8,128)(2,1)S(1)} %get-tuple-element.388) | copy-start | bytes 884740 | tf_op jit(solution)/shard_map/while
  100.2 2.3 %copy-start.7 = (bf16[3,2,192,128]{3,2,1,0:T(8,128)(2,1)}, bf16[3,2,192,128]{3,2,1,0:T(8,128)(2,1)S(1)}, u32[]{:S(2)}) copy-start(bf16[3,2,192,128]{3,2,1,0:T(8,128)(2,1)S(1)} %get-tuple-element.387) | copy-start | bytes 884740 | tf_op jit(solution)/shard_map/while
  105.7 2.2 %copy-start.1 = (bf16[4,192,192]{1,2,0:T(8,128)(2,1)S(1)}, bf16[4,192,192]{1,2,0:T(8,128)(2,1)}, u32[]{:S(2)}) copy-start(bf16[4,192,192]{1,2,0:T(8,128)(2,1)} %copy-done) | copy-start | bytes 884740 | tf_op jit(solution)/shard_map/while
  105.7 2.2 %copy-start.4 = (bf16[3,2,192,128]{3,2,1,0:T(8,128)(2,1)S(1)}, bf16[3,2,192,128]{3,2,1,0:T(8,128)(2,1)}, u32[]{:S(2)}) copy-start(bf16[3,2,192,128]{3,2,1,0:T(8,128)(2,1)} %copy-done.3) | copy-start | bytes 884740 | tf_op jit(solution)/shard_map/while
  105.7 2.2 %copy-start.6 = (bf16[3,2,192,128]{3,2,1,0:T(8,128)(2,1)S(1)}, bf16[3,2,192,128]{3,2,1,0:T(8,128)(2,1)}, u32[]{:S(2)}) copy-start(bf16[3,2,192,128]{3,2,1,0:T(8,128)(2,1)} %copy-done.5) | copy-start | bytes 884740 | tf_op jit(solution)/shard_map/while
  105.7 2.2 %copy-start.8 = (bf16[3,2,192,128]{3,2,1,0:T(8,128)(2,1)S(1)}, bf16[3,2,192,128]{3,2,1,0:T(8,128)(2,1)}, u32[]{:S(2)}) copy-start(bf16[3,2,192,128]{3,2,1,0:T(8,128)(2,1)} %copy-done.7) | copy-start | bytes 884740 | tf_op jit(solution)/shard_map/while
  108.4 8.6 %copy-start.9 = (bf16[3,2,192,128]{3,2,1,0:T(8,128)(2,1)S(1)}, bf16[3,2,192,128]{3,2,1,0:T(8,128)(2,1)}, u32[]{:S(2)}) copy-start(bf16[3,2,192,128]{3,2,1,0:T(8,128)(2,1)} %get-tuple-element.144) | copy-start | bytes 884740
  111.6 23.8 %all-to-all-start.7 = ((bf16[6,192,128]{2,0,1:T(8,128)(2,1)}), bf16[6,192,128]{2,0,1:T(8,128)(2,1)S(1)}, u32[]{:S(2)}, u32[]{:S(2)}) async-start(bf16[6,192,128]{2,0,1:T(8,128)(2,1)} %copy.135), calls=%async_computation.7 | async-start | bytes 786432 | tf_op jit(solution)/shard_map/all_to_all | solution.py:126
  135.4 12.3 %all-to-all-start.5 = ((bf16[6,192,128]{2,0,1:T(8,128)(2,1)}), bf16[6,192,128]{2,0,1:T(8,128)(2,1)S(1)}, u32[]{:S(2)}, u32[]{:S(2)}) async-start(bf16[6,192,128]{2,0,1:T(8,128)(2,1)} %copy.127), calls=%async_computation.5 | async-start | bytes 786432 | tf_op jit(solution)/shard_map/all_to_all | solution.py:120
  147.7 12.3 %all-to-all-start.6 = ((bf16[6,192,128]{2,0,1:T(8,128)(2,1)}), bf16[6,192,128]{2,0,1:T(8,128)(2,1)S(1)}, u32[]{:S(2)}, u32[]{:S(2)}) async-start(bf16[6,192,128]{2,0,1:T(8,128)(2,1)} %copy.131), calls=%async_computation.6 | async-start | bytes 786432 | tf_op jit(solution)/shard_map/all_to_all | solution.py:123
  151.2 38.8 %reduce-scatter.5.cloned.1.call-start = ((), (), s32[]{:S(2)}) async-start(), calls=%async_computation.10 | async-start | bytes 442368 | tf_op jit(solution)/shard_map/reduce_scatter | solution.py:131
  (3 other events, 2.7 us)
Sparse Core Ops, SparseCore 0:
  109.8 25.3 reduce-scatter.6
  155.6 34.3 reduce-scatter.4
